TPU v7x, 512 devices: a 4x2x32 block of a 4x8x32 slice. The times are simulated.
512 devices in a mesh: groups: 2 (over y), blk: 64 (over z, core), head: 4 (over x).
Axes of the slice: x: 4, y: 2, z: 32, core: 2. Of those that a mesh axis runs over, the one named last changes fastest.
The devices are a block of a 4x8x32 slice.
Arguments:
- queries: bfloat16 [4, 64, 8192], P('groups', 'blk', 'head'), parts along dimension 0, may hold values from -4.5 to 4.5
- stored_cache_keys: bfloat16 [4, 32768, 1024], P('groups', 'blk', 'head'), parts along dimension 0, may hold values from -4.5 to 4.5
- stored_cache_values: bfloat16 [4, 32768, 1024], P('groups', 'blk', 'head'), parts along dimension 0, may hold values from -6 to 6
- out_weight: bfloat16 [8192, 8192], P('head', 'blk'), may hold values from -3 to 3
- lengths: int32 [4], P('groups'), parts along dimension 0, may hold values from 16384 to 32768
Outputs:
- projected: bfloat16 [4, 64, 8192], P('groups', 'head', 'blk'), parts along dimension 0
There are 2 independent parts, one for each index of `groups`. A program takes and returns all parts, laid end to end along the dimension named above; an argument that names none is the same for every part. Nothing has to cross between parts.
All inputs are finite; a program needn't handle non-finite values.
Results may differ from a plain program's by a relative error of at most 0.0056.
Values may be sent and summed in bfloat16 or wider, within the bound.
No kernel may reach another device: no remote copies, remote signals or barrier semaphores. Data moves between devices by JAX's collectives and lax.ppermute only.
A program may use at most 64 MiB of HBM per device.

v0:
```python
import math
import jax
import jax.numpy as jnp
from jax import lax
from jax.sharding import Mesh
from jax.sharding import PartitionSpec as P

REQUEST_COUNT = 2
QUERY_HEAD_COUNT = 64
KEY_VALUE_HEADS = 8
HEAD_DIMENSION = 128
BLK = ("blk_0", "blk_1")
masked_fill_value = -1e30


def in_one_piece(arrays, axis, split_dim, concat_dim, along):
    ends, at = ([], 0)
    for a in arrays[:-1]:
        at += a.shape[along]
        ends.append(at)
    both = jnp.concatenate(arrays, axis=along)
    return tuple(
        jnp.split(
            lax.all_to_all(both, axis, split_axis=split_dim, concat_axis=concat_dim, tiled=True),
            ends,
            axis=along,
        )
    )


def joined_along(pieces, dim):
    shape = list(pieces.shape[1:])
    shape[dim] *= pieces.shape[0]
    return jnp.moveaxis(pieces, 0, dim).reshape(shape)


def gather_in_order(value, axes, order):
    pieces = value
    for k in order:
        pieces = lax.all_gather(pieces, axes[k])
    done = order[::-1]
    back = [done.index(k) for k in range(len(axes))]
    pieces = pieces.transpose(*back, *range(len(axes), pieces.ndim))
    return pieces.reshape(-1, *value.shape)


def gathered_by_axis(value, axes, order, dim):
    return joined_along(gather_in_order(value, axes, order), dim)


def in_blocks(value, dim, peers):
    before, after = (value.shape[:dim], value.shape[dim + 1 :])
    return jnp.moveaxis(value.reshape(*before, peers, -1, *after), dim, 0)


def sent_and_summed(value, axis, dim):
    pieces = in_blocks(value, dim, lax.axis_size(axis))
    arrived = lax.all_to_all(pieces, axis, split_axis=0, concat_axis=0, tiled=True)
    return arrived.sum(axis=0)


def body(queries, stored_cache_keys, stored_cache_values, out_weight, lengths):
    group_width = QUERY_HEAD_COUNT // KEY_VALUE_HEADS
    local_heads = stored_cache_keys.shape[2] // HEAD_DIMENSION
    query_heads = local_heads * group_width
    span = stored_cache_keys.shape[1]
    new_count = queries.shape[1] * lax.axis_size(BLK)
    key_pos = lax.axis_index(BLK) * span + jnp.arange(span, dtype=jnp.int32)
    score_scale = 1.0 / math.sqrt(HEAD_DIMENSION)
    piece = lax.all_gather(queries, BLK, axis=1, tiled=True)
    rows_count = piece.shape[1]
    query_pos = lengths[:, None] - new_count + jnp.arange(rows_count, dtype=jnp.int32)[None, :]
    sums_list = []
    maxima_list = []
    totals_list = []
    for request in range(REQUEST_COUNT):
        visible = (key_pos[None, :] <= query_pos[request][:, None])[:, None, :]
        parts_sum, parts_max, parts_total = ([], [], [])
        for kv_head in range(local_heads):
            block_query = piece[
                request,
                :,
                kv_head
                * group_width
                * HEAD_DIMENSION : (kv_head + 1)
                * group_width
                * HEAD_DIMENSION,
            ].reshape(rows_count, group_width, HEAD_DIMENSION)
            local_keys = stored_cache_keys[
                request, :, kv_head * HEAD_DIMENSION : (kv_head + 1) * HEAD_DIMENSION
            ]
            local_values = stored_cache_values[
                request, :, kv_head * HEAD_DIMENSION : (kv_head + 1) * HEAD_DIMENSION
            ]
            scores = (
                jnp.einsum(
                    "ngd,cd->ngc", block_query, local_keys, preferred_element_type=jnp.float32
                )
                * score_scale
            )
            block_max = jnp.max(jnp.where(visible, scores, masked_fill_value), axis=-1)
            weights = jnp.where(visible, jnp.exp(scores - block_max[..., None]), 0.0)
            parts_total.append(jnp.sum(weights, axis=-1))
            parts_max.append(block_max)
            weighted = jnp.einsum(
                "ngc,cd->ngd",
                weights.astype(jnp.bfloat16),
                local_values,
                preferred_element_type=jnp.float32,
            )
            parts_sum.append(weighted.reshape(rows_count, group_width * HEAD_DIMENSION))
        sums_list.append(jnp.concatenate(parts_sum, axis=1))
        maxima_list.append(jnp.concatenate(parts_max, axis=1))
        totals_list.append(jnp.concatenate(parts_total, axis=1))
    new_sums = jnp.stack(sums_list, axis=0)
    new_maxima = jnp.stack(maxima_list, axis=0)
    new_totals = jnp.stack(totals_list, axis=0)
    received = in_one_piece((new_sums[None], new_maxima[None], new_totals[None]), BLK, 2, 0, 3)
    part_sums, part_max, part_totals = received
    blocks = part_sums.shape[0]
    own_rows = part_sums.shape[2]
    top = jnp.max(part_max, axis=0)
    factor = jnp.exp(part_max - top[None])
    overall = jnp.sum(factor * part_totals, axis=0)
    shaped = part_sums.reshape(blocks, REQUEST_COUNT, own_rows, query_heads, HEAD_DIMENSION)
    merged = jnp.sum(shaped * factor[..., None], axis=0) / overall[..., None]
    own_attention = merged.astype(jnp.bfloat16).reshape(
        REQUEST_COUNT, own_rows, query_heads * HEAD_DIMENSION
    )
    terms = jnp.einsum(
        "rnc,cd->rnd",
        gathered_by_axis(own_attention, BLK, (0, 1), 1),
        out_weight,
        preferred_element_type=jnp.float32,
    )
    return sent_and_summed(terms, "head", 1).astype(jnp.bfloat16)


def solution(mesh):
    torus = Mesh(
        mesh.devices.reshape(mesh.shape["groups"], 32, 2, mesh.shape["head"]),
        ("groups", "blk_0", "blk_1", "head"),
    )
    return jax.shard_map(
        body,
        mesh=torus,
        in_specs=(
            P("groups", BLK, "head"),
            P("groups", BLK, "head"),
            P("groups", BLK, "head"),
            P("head", BLK),
            P("groups"),
        ),
        out_specs=P("groups", "head", BLK),
        check_vma=False,
    )
```

profile of v0, /device:TPU:40, one launch (start us, length us, event | category | flops | bytes accessed | tf_op | source)
XLA Modules:
  0.0 312.7 jit_solution(946098355099298313)
XLA Ops:
  0.0 0.0 copy-start
  0.0 0.7 broadcast_add_fusion
  0.7 0.1 iota_add_fusion.1
  0.8 97.1 %all_gather.12 = bf16[2,64,2048]{2,0,1:T(2,128)(2,1)S(1)} all-gather(bf16[2,1,2048]{2,0,1:T(2,128)(2,1)} %param.5), channel_id=1, replica_groups=mesh['groups'=2,'blk_0'=32,'blk_1'=2,'head'=4] {'blk_0','blk_1'}, dimensions={1}, use_global_device_ids=true | all-gather | bytes 532480 | tf_op jit(solution)/shard_map/all_gather | solution.py:70
  97.9 2.3 slice_reduce_fusion.3
  100.3 0.7 copy.35
  100.9 0.1 broadcast_compare_fusion.1
  101.0 1.3 select_reduce_fusion.1
  102.4 0.1 copy.20
  102.5 1.3 fusion.11
  103.7 2.1 fusion.5
  105.9 0.1 copy.21
  105.9 1.3 fusion.9
  107.2 1.3 select_reduce_fusion.3
  108.6 0.0 copy-start.1
  108.6 0.0 copy-start.2
  108.6 0.1 copy.18
  108.7 1.4 fusion.15
  110.1 0.0 copy-done.1
  110.1 0.0 copy-done.2
  110.1 2.6 fusion.1
  112.7 0.1 copy.19
  112.8 1.3 fusion.3
  114.1 0.0 copy-start.5
  114.1 1.3 fusion.13
  115.4 0.0 copy-done.5
  115.4 0.1 copy.25
  115.5 0.1 copy_bitcast_fusion
  115.6 0.0 copy-start.6
  115.6 0.0 copy-start.4
  115.6 0.0 copy-start.3
  115.7 0.4 stack.28
  116.0 0.3 copy-done.6
  116.4 0.1 copy.23
  116.4 0.0 copy-done.4
  116.4 0.1 copy.24
  116.5 0.0 copy-done.3
  116.5 0.1 copy.26
  116.6 0.1 copy_bitcast_fusion.2
  116.7 0.4 stack.27
  117.1 0.1 copy.22
  117.2 0.1 copy.27
  117.3 0.9 maximum_bitcast_fusion
  118.3 2.1 concatenate.27
  120.4 121.5 %all_to_all.23 = f32[1,2,64,2080]{3,1,0,2:T(2,128)S(1)} all-to-all(f32[1,2,64,2080]{3,1,0,2:T(2,128)S(1)} %concatenate.27), channel_id=1, replica_groups=mesh['groups'=2,'blk_0'=32,'blk_1'=2,'head'=4] {'blk_0','blk_1'}, dimensions={2} | all-to-all | bytes 2129920 | tf_op jit(solution)/shard_map/all_to_all | solution.py:24
  241.9 0.1 slice_reduce_fusion.4
  242.0 0.1 fusion.47
  242.1 0.1 div.19
  242.2 1.3 mul.43
  243.6 1.8 mul.44
  245.3 0.6 fusion
  245.9 52.8 %all_gather.13 = bf16[32,2,1,2048]{3,1,2,0:T(2,128)(2,1)S(1)} all-gather(bf16[1,2,1,2048]{3,1,2,0:T(2,128)(2,1)S(1)} %fusion.48), channel_id=1, replica_groups=mesh['groups'=2,'blk_0'=32,'blk_1'=2,'head'=4] {'blk_0'}, dimensions={0}, use_global_device_ids=true | all-gather | bytes 270336 | tf_op jit(solution)/shard_map/all_gather | solution.py:40
  298.7 0.1 copy.28
  298.8 2.2 all-gather
  301.0 0.5 copy.29
  301.6 0.2 copy.30
  301.7 0.0 copy-done
  301.7 0.3 convolution_bitcast_fusion
  302.1 10.0 %all_to_all.24 = f32[4,2,16,128]{3,2,1,0:T(8,128)S(1)} all-to-all(f32[4,2,16,128]{3,2,1,0:T(8,128)S(1)} %copy.31), channel_id=1, replica_groups=mesh['groups'=2,'blk_0'=32,'blk_1'=2,'head'=4] {'head'}, dimensions={0} | all-to-all | bytes 131072 | tf_op jit(solution)/shard_map/all_to_all | solution.py:58
  312.1 0.6 reduce_sum.72
  (15 shorter events, 0.2 us)
Async XLA Ops:
  0.0 301.7 %copy-start = (bf16[2048,128]{1,0:T(8,128)(2,1)S(1)}, bf16[2048,128]{1,0:T(8,128)(2,1)}, u32[]{:S(2)}) copy-start(bf16[2048,128]{1,0:T(8,128)(2,1)} %param.8) | copy-start | bytes 1572868
  108.6 1.5 copy-start.1
  108.6 1.5 copy-start.2
  114.1 1.3 copy-start.5
  115.6 0.8 copy-start.6
  115.6 0.8 copy-start.4
  115.6 0.9 copy-start.3
where the time goes:
time: 313 us
  blocking collectives  284 us (91%)
  matrix products  13 us (4%)
  local copies, waits for them, and re-layouts  11 us (4%)
  other arithmetic  4.7 us (2%)
    all_to_all x1, blocking collectives, in_one_piece(): lax.all_to_all(both, axis, split_axis=split_dim, concat_axis=concat_dim,...  121 us
    all_gather x1, blocking collectives, body(): piece = lax.all_gather(queries, BLK, axis=1, tiled=True)  97.1 us
    all_gather x2, blocking collectives, gather_in_order(): pieces = lax.all_gather(pieces, axes[k])  55 us
    all_to_all x1, blocking collectives, sent_and_summed(): lax.all_to_all(pieces, axis, split_axis=0, concat_axis=0, tiled=True)  10 us
    dot_general x4, matrix products, body(): jnp.einsum('ngd,cd->ngc', block_query, local_keys, preferred_element_type...  7.44 us

commit v1 on v0

--- a/solution.py
+++ b/solution.py
@@ -67,7 +67,8 @@
     new_count = queries.shape[1] * lax.axis_size(BLK)
     key_pos = lax.axis_index(BLK) * span + jnp.arange(span, dtype=jnp.int32)
     score_scale = 1.0 / math.sqrt(HEAD_DIMENSION)
-    piece = lax.all_gather(queries, BLK, axis=1, tiled=True)
+    sent = jnp.stack([queries] * lax.axis_size(BLK))
+    piece = jnp.concatenate(lax.all_to_all(sent, BLK, 0, 0), axis=1)
     rows_count = piece.shape[1]
     query_pos = lengths[:, None] - new_count + jnp.arange(rows_count, dtype=jnp.int32)[None, :]
     sums_list = []

time: 313 us -> 328 us (1.048)
  blocking collectives: 284 us -> 186 us
  waiting for transfers between devices: 0 us -> 64 us
  starting transfers between devices: 0 us -> 47.3 us
    all_gather x1 -> x0, blocking collectives: 97.1 us -> none  [body(): piece = lax.all_gather(queries, BLK, axis=1, tiled=True)]
    all_to_all x0 -> x1, waiting for transfers between devices: none -> 64 us  [body(): piece = jnp.concatenate(lax.all_to_all(sent, BLK, 0, 0), axis=1)]
    all_to_all x0 -> x1, starting transfers between devices: none -> 47.3 us  [body(): piece = jnp.concatenate(lax.all_to_all(sent, BLK, 0, 0), axis=1)]
  transfers between devices with their start and end apart: 0 -> 1, of which waited for: 0 -> 1; matrix products, arithmetic and copies ran while one was open for 0% -> 0% of each run, Pallas kernels for 0% -> 0%
where the time goes in v1:
time: 328 us
  blocking collectives  186 us (57%)
  waiting for transfers between devices  64 us (20%)
  starting transfers between devices  47.3 us (14%)
  matrix products  13 us (4%)
  local copies, waits for them, and re-layouts  12.9 us (4%)
  other arithmetic  3.99 us (1%)
    all_to_all x1, blocking collectives, in_one_piece(): lax.all_to_all(both, axis, split_axis=split_dim, concat_axis=concat_dim,...  121 us
    all_to_all x1, waiting for transfers between devices, body(): piece = jnp.concatenate(lax.all_to_all(sent, BLK, 0, 0), axis=1)  64 us
    all_gather x2, blocking collectives, gather_in_order(): pieces = lax.all_gather(pieces, axes[k])  55.5 us
    all_to_all x1, starting transfers between devices, body(): piece = jnp.concatenate(lax.all_to_all(sent, BLK, 0, 0), axis=1)  47.3 us
    all_to_all x1, blocking collectives, sent_and_summed(): lax.all_to_all(pieces, axis, split_axis=0, concat_axis=0, tiled=True)  10 us
    dot_general x4, matrix products, body(): jnp.einsum('ngd,cd->ngc', block_query, local_keys, preferred_element_type...  7.43 us
  transfers between devices with their start and end apart: 1, of which 1 were waited for; matrix products, arithmetic and copies ran while one was open for 0% of the time, Pallas kernels for 0%

profile of v1, /device:TPU:40, one launch (start us, length us, event | category | flops | bytes accessed | tf_op | source)
XLA Modules:
  0.0 327.7 jit_solution(6491753173265659519)
XLA Ops:
  0.0 0.0 copy-start
  0.0 0.0 copy-start.7
  0.0 1.8 stack.20
  1.8 47.3 %all-to-all-start = ((bf16[64,2,1,2048]{3,1,2,0:T(2,128)(2,1)}), bf16[64,2,1,2048]{3,1,2,0:T(2,128)(2,1)S(1)}, u32[]{:S(2)}, u32[]{:S(2)}) async-start(bf16[64,2,1,2048]{3,1,2,0:T(2,128)(2,1)} %stack.20), calls=%async_computation | async-start | bytes 1048576 | tf_op jit(solution)/shard_map/all_to_all | solution.py:71
  49.2 0.0 copy-done.7
  49.2 0.1 iota_add_fusion.1
  49.3 0.1 broadcast_compare_fusion.1
  49.4 64.0 %all-to-all-done = bf16[64,2,1,2048]{3,1,2,0:T(2,128)(2,1)S(1)} async-done(((bf16[64,2,1,2048]{3,1,2,0:T(2,128)(2,1)}), bf16[64,2,1,2048]{3,1,2,0:T(2,128)(2,1)S(1)}, u32[]{:S(2)}, u32[]{:S(2)}) %all-to-all-start) | async-done | bytes 524320 | tf_op jit(solution)/shard_map/all_to_all | solution.py:71
  113.4 2.3 slice_reduce_fusion.3
  115.7 0.7 copy.45
  116.4 1.3 select_reduce_fusion.1
  117.7 0.1 copy.30
  117.8 1.3 fusion.11
  119.1 2.1 fusion.5
  121.2 0.1 copy.31
  121.3 1.3 fusion.9
  122.6 1.3 select_reduce_fusion.3
  123.9 0.0 copy-start.1
  123.9 0.0 copy-start.2
  123.9 0.1 copy.28
  124.0 1.4 fusion.15
  125.5 0.0 copy-done.1
  125.5 0.0 copy-done.2
  125.5 2.6 fusion.1
  128.1 0.1 copy.29
  128.1 1.3 fusion.3
  129.5 0.0 copy-start.5
  129.5 1.3 fusion.13
  130.8 0.0 copy-done.5
  130.8 0.1 copy.35
  130.8 0.1 copy_bitcast_fusion
  131.0 0.0 copy-start.6
  131.0 0.0 copy-start.4
  131.0 0.0 copy-start.3
  131.0 0.4 stack.22
  131.4 0.3 copy-done.6
  131.7 0.1 copy.33
  131.8 0.0 copy-done.4
  131.8 0.1 copy.34
  131.8 0.0 copy-done.3
  131.8 0.1 copy.36
  131.9 0.1 copy_bitcast_fusion.2
  132.1 0.4 stack.21
  132.5 0.1 copy.32
  132.6 0.1 copy.37
  132.7 0.9 maximum_bitcast_fusion
  133.6 2.1 concatenate.27
  135.8 120.7 %all_to_all.28 = f32[1,2,64,2080]{3,1,0,2:T(2,128)S(1)} all-to-all(f32[1,2,64,2080]{3,1,0,2:T(2,128)S(1)} %concatenate.27), channel_id=1, replica_groups=mesh['groups'=2,'blk_0'=32,'blk_1'=2,'head'=4] {'blk_0','blk_1'}, dimensions={2} | all-to-all | bytes 2129920 | tf_op jit(solution)/shard_map/all_to_all | solution.py:24
  256.5 0.1 slice_reduce_fusion.4
  256.6 0.1 fusion.47
  256.7 0.1 div.19
  256.8 1.3 mul.43
  258.1 1.8 mul.44
  259.9 0.6 fusion
  260.5 53.3 %all_gather.9 = bf16[32,2,1,2048]{3,1,2,0:T(2,128)(2,1)S(1)} all-gather(bf16[1,2,1,2048]{3,1,2,0:T(2,128)(2,1)S(1)} %fusion.48), channel_id=1, replica_groups=mesh['groups'=2,'blk_0'=32,'blk_1'=2,'head'=4] {'blk_0'}, dimensions={0}, use_global_device_ids=true | all-gather | bytes 270336 | tf_op jit(solution)/shard_map/all_gather | solution.py:40
  313.7 0.1 copy.38
  313.8 2.2 all-gather
  316.1 0.5 copy.39
  316.6 0.2 copy.40
  316.8 0.0 copy-done
  316.8 0.3 convolution_bitcast_fusion
  317.1 10.0 %all_to_all.29 = f32[4,2,16,128]{3,2,1,0:T(8,128)S(1)} all-to-all(f32[4,2,16,128]{3,2,1,0:T(8,128)S(1)} %copy.41), channel_id=1, replica_groups=mesh['groups'=2,'blk_0'=32,'blk_1'=2,'head'=4] {'head'}, dimensions={0} | all-to-all | bytes 131072 | tf_op jit(solution)/shard_map/all_to_all | solution.py:58
  327.1 0.6 reduce_sum.72
  (16 shorter events, 0.2 us)
Async XLA Ops:
  0.0 316.8 %copy-start = (bf16[2048,128]{1,0:T(8,128)(2,1)S(1)}, bf16[2048,128]{1,0:T(8,128)(2,1)}, u32[]{:S(2)}) copy-start(bf16[2048,128]{1,0:T(8,128)(2,1)} %param.8) | copy-start | bytes 1572868
  0.0 49.2 %copy-start.7 = (s32[2]{0:T(128)S(1)}, s32[2]{0:T(128)}, u32[]{:S(2)}) copy-start(s32[2]{0:T(128)} %param.9) | copy-start | bytes 28
  1.8 111.6 %all-to-all-start = ((bf16[64,2,1,2048]{3,1,2,0:T(2,128)(2,1)}), bf16[64,2,1,2048]{3,1,2,0:T(2,128)(2,1)S(1)}, u32[]{:S(2)}, u32[]{:S(2)}) async-start(bf16[64,2,1,2048]{3,1,2,0:T(2,128)(2,1)} %stack.20), calls=%async_computation | async-start | bytes 1048576 | tf_op jit(solution)/shard_map/all_to_all | solution.py:71
  123.9 1.5 copy-start.1
  123.9 1.5 copy-start.2
  129.5 1.3 copy-start.5
  131.0 0.8 copy-start.6
  131.0 0.8 copy-start.4
  131.0 0.9 copy-start.3
